TPU v7x, 512 devices: a whole 4x8x8 slice. The times are simulated.
512 devices in a mesh: dp: 128 (over z, y, core), tensor: 4 (over x).
Axes of the slice: x: 4, y: 8, z: 8, core: 2. Of those that a mesh axis runs over, the one named last changes fastest.
Arguments:
- hidden: bfloat16 [512, 8, 3584], P('dp', None, 'tensor')
- norm_gain: float32 [3584], replicated, may hold values from 0.5 to 2
- head_weight: bfloat16 [152064, 3584], P(('dp', 'tensor'))
- counts: int32 [128], P('dp'), may hold values from 1 to 3, as said below
- destination: int32 [512], P('dp'), may hold values from 0 to 127, as said below
- lengths: int32 [512], P('dp'), may hold values from 1 to 8
- labels: int32 [512, 8], P('dp'), may hold values from 0 to 152063
Outputs:
- scores: float32 [256], P('dp')
Inputs may be any that keep to these rules, and one draw needn't show every extreme that they name: The first counts[i] slots of index i are live; the counts sum to 256. The live slots of index i go to i or to i + 1, lower slots first to i; every index of dp is the destination of exactly 2 live slots; at most 1 live slots of one index go to the next index, a bound reached in every draw; entries of slots that are not live are arbitrary.
All inputs are finite; a program needn't handle non-finite values.
Results may differ from a plain program's by a relative error of at most 0.0025.
Values may be sent and summed in bfloat16 or wider, within the bound.
No kernel may reach another device: no remote copies, remote signals or barrier semaphores. Data moves between devices by JAX's collectives and lax.ppermute only.
A program may use at most 64 MiB of HBM per device.

v0:
```python
import jax
import jax.numpy as jnp
from jax import lax
from jax.sharding import Mesh
from jax.sharding import PartitionSpec as P

BLK_DEV = 2
DP = ("dp_0", "dp_1", "dp_2")
DP_TENSOR = ("dp_0", "dp_1", "dp_2", "tensor")
epsilon = 1e-06


def from_behind(block, axis, distance):
    devices = range(lax.axis_size(axis))
    route = [(i - distance, i) for i in devices if i - distance in devices]
    return lax.ppermute(block, axis, route)


def from_everyone(shard, axis):
    copies = jnp.broadcast_to(shard, (lax.axis_size(axis), *shard.shape))
    return lax.all_to_all(copies, axis, split_axis=0, concat_axis=0, tiled=True)


def in_order(tiles, dim):
    lengths = list(tiles.shape[1:])
    lengths[dim] *= tiles.shape[0]
    return jnp.moveaxis(tiles, 0, dim).reshape(lengths)


def collect(shard, axis, dim):
    tiles = from_everyone(shard, axis)
    return in_order(tiles, dim)


def by_axis(shard, axes):
    for axis in axes:
        shard = lax.pmax(shard, axis)
    return shard


def taken_together(shard, axis):
    return from_everyone(shard, axis).sum(axis=0)


def normalize(rows, norm_gain):
    values = rows.astype(jnp.float32)
    mean_square = jnp.mean(values * values, axis=-1, keepdims=True)
    return (values * lax.rsqrt(mean_square + epsilon) * norm_gain).astype(jnp.bfloat16)


def make_absorb(weight, vocab_start):

    def absorb(running, incoming, offset_row):
        rows, row_labels = incoming
        logits = lax.dot_general(
            rows, weight, (((1,), (1,)), ((), ())), preferred_element_type=jnp.float32
        )
        row_peak = jnp.max(logits, axis=1)
        scaled = jnp.exp(logits - row_peak[:, None])
        vocab_ids = vocab_start + jnp.arange(weight.shape[0], dtype=jnp.int32)
        hit = vocab_ids[None, :] == row_labels[:, None]
        fresh = (
            row_peak,
            jnp.sum(scaled, axis=1),
            jnp.sum(scaled * scaled, axis=1),
            jnp.sum(jnp.where(hit, logits, 0.0), axis=1),
        )
        return tuple((new for new in fresh))

    return absorb


def empty_stats(length):
    return tuple((jnp.zeros((length,), jnp.float32) for index in range(4)))


def earlier_count(flags):
    total = flags.shape[0]
    slot_ids = jnp.arange(total, dtype=jnp.int32)
    before = flags[None, :] & (slot_ids[None, :] < slot_ids[:, None])
    return jnp.sum(before, axis=1)


def per_device(hidden, norm_gain, head_weight, counts, destination, lengths, labels):
    capacity, block_len, quarter_width = hidden.shape
    peer_count = lax.axis_size(DP)
    tensor_ways = lax.axis_size("tensor")
    received_blocks = BLK_DEV
    spill_slots = BLK_DEV - 1
    dp_index = lax.axis_index(DP)
    tensor_index = lax.axis_index("tensor")
    slot_ids = jnp.arange(capacity, dtype=jnp.int32)
    is_live = slot_ids < counts[0]
    leaving = is_live & (destination == dp_index + 1)
    staying = is_live & (destination == dp_index)
    leave_rank = earlier_count(leaving)
    stay_rank = earlier_count(staying)
    flat_hidden = hidden.reshape(capacity, block_len * quarter_width)
    send_pick = (
        jnp.arange(spill_slots, dtype=jnp.int32)[:, None] == leave_rank[None, :]
    ) & leaving[None, :]
    packed = jnp.dot(
        send_pick.astype(jnp.bfloat16), flat_hidden, preferred_element_type=jnp.float32
    ).astype(jnp.bfloat16)
    packed_labels = jnp.sum(jnp.where(send_pick[:, :, None], labels[None, :, :], 0), axis=1)
    packed_lengths = jnp.sum(jnp.where(send_pick, lengths[None, :], 0), axis=1)
    occupied = jnp.sum(send_pick, axis=1)
    arrived, arrived_labels, arrived_lengths, arrived_occupied = from_behind(
        (packed, packed_labels, packed_lengths, occupied), DP, 1
    )
    incoming = jnp.sum(arrived_occupied).astype(jnp.int32)
    final_ids = jnp.arange(received_blocks, dtype=jnp.int32)
    place_in = (final_ids[:, None] == jnp.arange(spill_slots, dtype=jnp.int32)[None, :]) & (
        arrived_occupied > 0
    )[None, :]
    place_own = (final_ids[:, None] == (incoming + stay_rank)[None, :]) & staying[None, :]
    local = jnp.dot(place_in.astype(jnp.bfloat16), arrived, preferred_element_type=jnp.float32)
    local = local + jnp.dot(
        place_own.astype(jnp.bfloat16), flat_hidden, preferred_element_type=jnp.float32
    )
    local = local.astype(jnp.bfloat16).reshape(received_blocks * block_len, quarter_width)
    local_labels = jnp.sum(
        jnp.where(place_in[:, :, None], arrived_labels[None, :, :], 0), axis=1
    ) + jnp.sum(jnp.where(place_own[:, :, None], labels[None, :, :], 0), axis=1)
    local_labels = local_labels.reshape(-1).astype(jnp.int32)
    local_lengths = jnp.sum(jnp.where(place_in, arrived_lengths[None, :], 0), axis=1) + jnp.sum(
        jnp.where(place_own, lengths[None, :], 0), axis=1
    )
    local_lengths = local_lengths.astype(jnp.int32)
    token_count = received_blocks * block_len
    share = token_count // tensor_ways
    vocab_rows = head_weight.shape[0]
    gathered = collect(local, "tensor", 1)
    normed = normalize(gathered, norm_gain)
    absorb = make_absorb(head_weight, (dp_index * tensor_ways + tensor_index) * vocab_rows)
    row_peak, exp_sum, square_sum, label_logit = absorb(
        empty_stats(peer_count * token_count),
        (
            lax.all_gather(normed, DP, axis=0, tiled=True),
            lax.all_gather(local_labels, DP, axis=0, tiled=True),
        ),
        jnp.int32(0),
    )
    global_peak = by_axis(row_peak, DP_TENSOR)
    rescale = jnp.exp(row_peak - global_peak)
    exp_sum, square_sum, label_logit = (
        lax.psum_scatter(exp_sum * rescale, DP_TENSOR, scatter_dimension=0, tiled=True),
        lax.psum_scatter(
            square_sum * rescale * rescale, DP_TENSOR, scatter_dimension=0, tiled=True
        ),
        lax.psum_scatter(label_logit, DP_TENSOR, scatter_dimension=0, tiled=True),
    )
    own_peak = lax.dynamic_slice_in_dim(
        global_peak, (dp_index * tensor_ways + tensor_index) * share, share
    )
    token_error = (
        square_sum / (exp_sum * exp_sum) - 2.0 * jnp.exp(label_logit - own_peak) / exp_sum + 1.0
    )
    position = tensor_index * share + jnp.arange(share, dtype=jnp.int32)
    owner = (
        jnp.arange(received_blocks, dtype=jnp.int32)[:, None] == (position // block_len)[None, :]
    )
    token_length = jnp.sum(jnp.where(owner, local_lengths[:, None], 0), axis=0)
    counted = jnp.where(position % block_len < token_length, token_error, 0.0)
    partial_sum = jnp.sum(jnp.where(owner, counted[None, :], 0.0), axis=1)
    totals = taken_together(partial_sum, "tensor")
    return totals / local_lengths.astype(jnp.float32)


def solution(mesh):
    finer = Mesh(
        mesh.devices.reshape(8, 8, 2, mesh.shape["tensor"]), ("dp_0", "dp_1", "dp_2", "tensor")
    )
    placed = (P(DP, None, "tensor"), P(), P(DP_TENSOR, None), P(DP), P(DP), P(DP), P(DP, None))
    return jax.shard_map(per_device, mesh=finer, in_specs=placed, out_specs=P(DP), check_vma=False)
```

profile of v0, /device:TPU:24, one launch (start us, length us, event | category | flops | bytes accessed | tf_op | source)
XLA Modules:
  0.0 296.8 jit_solution(11436306540069125314)
XLA Ops:
  7.4 0.7 compare_and_fusion.3
  8.1 1.3 select_reduce_fusion.6
  9.4 1.9 collective-permute-start
  11.4 0.8 copy.14
  12.4 4.8 %collective-permute-start.2 = (bf16[1,7168]{1,0:T(2,128)(2,1)S(1)}, bf16[1,7168]{1,0:T(2,128)(2,1)S(1)}, u32[]{:S(2)}, u32[]{:S(2)}) collective-permute-start(bf16[1,7168]{1,0:T(2,128)(2,1)S(1)} %convert_element_type.45), channel_id=1, source_target_pairs={{0,4},{4,8},{8,12},{12,16},{16,20},{20,24},{24,28},{28,32},{32,36}... | collective-permute-start | bytes 43016 | tf_op jit(solution)/shard_map/ppermute | solution.py:16
  17.3 0.7 broadcast_add_fusion
  18.0 0.8 select_reduce_fusion.5
  19.8 10.0 %all_to_all.11 = bf16[4,16,896]{2,1,0:T(8,128)(2,1)S(1)} all-to-all(bf16[4,16,896]{2,1,0:T(8,128)(2,1)S(1)} %broadcast_in_dim.150), channel_id=1, replica_groups=mesh['dp_0'=8,'dp_1'=8,'dp_2'=2,'tensor'=4] {'tensor'}, dimensions={0} | all-to-all | bytes 229376 | tf_op jit(solution)/shard_map/all_to_all | solution.py:21
  30.0 1.4 multiply_convert_fusion
  31.4 0.8 select_reduce_fusion.2
  32.2 1.9 collective-permute-start.3
  34.1 4.1 %collective-permute-start.1 = (s32[1]{0:T(128)}, s32[1]{0:T(128)}, u32[]{:S(2)}, u32[]{:S(2)}) collective-permute-start(s32[1]{0:T(128)} %bitcast.3), channel_id=1, source_target_pairs={{0,4},{4,8},{8,12},{12,16},{16,20},{20,24},{24,28},{28,32},{32,36}... | collective-permute-start | bytes 20 | tf_op jit(solution)/shard_map/ppermute | solution.py:16
  38.2 1.3 dynamic-slice
  41.4 30.5 %all-reduce = s32[2048]{0:T(1024)S(1)} all-reduce(s32[2048]{0:T(1024)S(1)} %add_dynamic-update-slice_fusion), channel_id=1, replica_groups=mesh['dp_0'=8,'dp_1'=8,'dp_2'=2,'tensor'=4] {'dp_0','dp_1','dp_2'}, use_global_device_ids=true, to_apply=%add | all-reduce | flops 2048 | bytes 16384
  71.9 57.0 %all-gather.2.cloned.1.call-done = bf16[2048,3584]{1,0:T(8,128)(2,1)} async-done(((bf16[16,3584]{1,0:T(8,128)(2,1)}), bf16[2048,3584]{1,0:T(8,128)(2,1)}) %all-gather.2.cloned.1.call-update) | async-done | bytes 14680080 | tf_op jit(solution)/shard_map/all_gather | solution.py:139
  128.9 9.6 %fusion.9 = (f32[2048]{0:T(1024)S(1)}, f32[2048,297]{0,1:T(8,128)}) fusion(bf16[2048,3584]{1,0:T(8,128)(2,1)} %all-gather.2.cloned.1.call-done, bf16[297,3584]{1,0:T(8,128)(2,1)S(1)} %copy-done), kind=kOutput, calls=%fused_computation.51 | convolution fusion | flops 4360585216 | bytes 19250176 | tf_op jit(solution)/shard_map/dot_general | solution.py:55
  138.5 16.5 %pmax.28 = f32[2048]{0:T(1024)S(1)} all-reduce(f32[2048]{0:T(1024)S(1)} %get-tuple-element.20), channel_id=1, replica_groups=mesh['dp_0'=8,'dp_1'=8,'dp_2'=2,'tensor'=4] {'dp_0'}, use_global_device_ids=true, to_apply=%region_9.10 | all-reduce | flops 2048 | bytes 16384 | tf_op jit(solution)/shard_map/pmax | solution.py:37
  155.0 14.7 %pmax.29 = f32[2048]{0:T(1024)S(1)} all-reduce(f32[2048]{0:T(1024)S(1)} %pmax.28), channel_id=1, replica_groups=mesh['dp_0'=8,'dp_1'=8,'dp_2'=2,'tensor'=4] {'dp_1'}, use_global_device_ids=true, to_apply=%region_10.11 | all-reduce | flops 2048 | bytes 16384 | tf_op jit(solution)/shard_map/pmax | solution.py:37
  169.6 2.5 pmax.30
  172.1 10.5 %pmax.31 = f32[2048]{0:T(1024)S(1)} all-reduce(f32[2048]{0:T(1024)S(1)} %pmax.30), channel_id=1, replica_groups=mesh['dp_0'=8,'dp_1'=8,'dp_2'=2,'tensor'=4] {'tensor'}, use_global_device_ids=true, to_apply=%region_12.13 | all-reduce | flops 2048 | bytes 16384 | tf_op jit(solution)/shard_map/pmax | solution.py:37
  182.7 2.5 fusion
  185.2 94.9 %all-reduce.4 = (f32[2048]{0:T(1024)S(1)}, f32[2048]{0:T(1024)S(1)}, f32[2048]{0:T(1024)S(1)}) all-reduce(f32[2048]{0:T(1024)S(1)} %get-tuple-element.7, f32[2048]{0:T(1024)S(1)} %get-tuple-element.17, f32[2048]{0:T(1024)S(1)} %get-tuple-element.16), channel_id=4, replica_groups=mesh['dp_0'=8,'dp_1'=8,'dp_2'=2,'tensor'=4] {'dp_0','dp_1','dp_2','tensor'}, use_global_device_ids=true, to_apply=%region_19.20.clone | all-reduce | flops 6144 | bytes 49152
  280.3 8.4 %all_to_all.12 = f32[4,1,2]{2,1,0:T(1,128)S(1)} all-to-all(f32[4,1,2]{2,1,0:T(1,128)S(1)} %broadcast_in_dim.163), channel_id=1, replica_groups=mesh['dp_0'=8,'dp_1'=8,'dp_2'=2,'tensor'=4] {'tensor'}, dimensions={0} | all-to-all | bytes 64 | tf_op jit(solution)/shard_map/all_to_all | solution.py:21
  288.8 1.2 convert_divide_fusion
  (40 shorter events, 2.3 us)
Async XLA Ops:
  6.5 122.4 %copy-start = (bf16[297,3584]{1,0:T(8,128)(2,1)S(1)}, bf16[297,3584]{1,0:T(8,128)(2,1)}, u32[]{:S(2)}) copy-start(bf16[297,3584]{1,0:T(8,128)(2,1)} %param.9) | copy-start | bytes 6386692
  6.5 33.7 %copy-start.1 = (s32[4,8]{1,0:T(4,128)S(1)}, s32[4,8]{1,0:T(4,128)}, u32[]{:S(2)}) copy-start(s32[4,8]{1,0:T(4,128)} %param.13) | copy-start | bytes 388
  6.5 122.4 %all-gather.2.cloned.1.call-start = ((), (), s32[]{:S(2)}) async-start(), calls=%async_computation.2 | async-start | bytes 14794752 | tf_op jit(solution)/shard_map/all_gather | solution.py:139
  9.4 7.9 %collective-permute-start = (s32[1]{0:T(128)}, s32[1]{0:T(128)}, u32[]{:S(2)}, u32[]{:S(2)}) collective-permute-start(s32[1]{0:T(128)} %bitcast.1), channel_id=1, source_target_pairs={{0,4},{4,8},{8,12},{12,16},{16,20},{20,24},{24,28},{28,32},{32,36}... | collective-permute-start | bytes 20 | tf_op jit(solution)/shard_map/ppermute | solution.py:16
  12.4 7.1 %collective-permute-start.2 = (bf16[1,7168]{1,0:T(2,128)(2,1)S(1)}, bf16[1,7168]{1,0:T(2,128)(2,1)S(1)}, u32[]{:S(2)}, u32[]{:S(2)}) collective-permute-start(bf16[1,7168]{1,0:T(2,128)(2,1)S(1)} %convert_element_type.45), channel_id=1, source_target_pairs={{0,4},{4,8},{8,12},{12,16},{16,20},{20,24},{24,28},{28,32},{32,36}... | collective-permute-start | bytes 43016 | tf_op jit(solution)/shard_map/ppermute | solution.py:16
  32.2 8.9 %collective-permute-start.3 = (s32[1,8]{1,0:T(1,128)S(1)}, s32[1,8]{1,0:T(1,128)S(1)}, u32[]{:S(2)}, u32[]{:S(2)}) collective-permute-start(s32[1,8]{1,0:T(1,128)S(1)} %bitcast.36), channel_id=1, source_target_pairs={{0,4},{4,8},{8,12},{12,16},{16,20},{20,24},{24,28},{28,32},{32,36}... | collective-permute-start | bytes 104 | tf_op jit(solution)/shard_map/ppermute | solution.py:16
  34.1 6.3 %collective-permute-start.1 = (s32[1]{0:T(128)}, s32[1]{0:T(128)}, u32[]{:S(2)}, u32[]{:S(2)}) collective-permute-start(s32[1]{0:T(128)} %bitcast.3), channel_id=1, source_target_pairs={{0,4},{4,8},{8,12},{12,16},{16,20},{20,24},{24,28},{28,32},{32,36}... | collective-permute-start | bytes 20 | tf_op jit(solution)/shard_map/ppermute | solution.py:16
Sparse Core Ops, SparseCore 0:
  31.6 97.3 all-gather.1
where the time goes:
time: 297 us
  blocking collectives  188 us (63%)
  waiting for transfers between devices  57 us (19%)
  between operations  15.8 us (5%)
  starting transfers between devices  12.7 us (4%)
  other arithmetic  11 us (4%)
  matrix products  9.88 us (3%)
    unnamed x2, blocking collectives  125 us
    all_gather x1, waiting for transfers between devices, per_device(): lax.all_gather(normed, DP, axis=0, tiled=True)  57 us
    pmax x4, blocking collectives, by_axis(): shard = lax.pmax(shard, axis)  44.1 us
    all_to_all x2, blocking collectives, from_everyone(): return lax.all_to_all(copies, axis, split_axis=0, concat_axis=0, tiled=True)  18.4 us
    ppermute x4, starting transfers between devices, from_behind(): return lax.ppermute(block, axis, route)  12.7 us
    dot_general x1, matrix products, absorb(): lax.dot_general(rows, weight, (((1,), (1,)), ((), ())), preferred_element...  9.57 us
  transfers between devices with their start and end apart: 5, of which 1 were waited for; matrix products, arithmetic and copies ran while one was open for 2% of the time, Pallas kernels for 0%

commit v1 on v0

--- a/solution.py
+++ b/solution.py
@@ -8,6 +8,13 @@
 DP = ("dp_0", "dp_1", "dp_2")
 DP_TENSOR = ("dp_0", "dp_1", "dp_2", "tensor")
 epsilon = 1e-06
+
+
+def exchange_gather(x, mesh_axis, along):
+    devices = lax.axis_size(mesh_axis)
+    blocks = jnp.stack([x for _ in range(devices)])
+    blocks = lax.all_to_all(blocks, mesh_axis, split_axis=0, concat_axis=0)
+    return jnp.concatenate(blocks, axis=along)
 
 
 def from_behind(block, axis, distance):
@@ -135,10 +142,7 @@
     absorb = make_absorb(head_weight, (dp_index * tensor_ways + tensor_index) * vocab_rows)
     row_peak, exp_sum, square_sum, label_logit = absorb(
         empty_stats(peer_count * token_count),
-        (
-            lax.all_gather(normed, DP, axis=0, tiled=True),
-            lax.all_gather(local_labels, DP, axis=0, tiled=True),
-        ),
+        (exchange_gather(normed, DP, 0), lax.all_gather(local_labels, DP, axis=0, tiled=True)),
         jnp.int32(0),
     )
     global_peak = by_axis(row_peak, DP_TENSOR)

time: 297 us -> 692 us (2.33)
  the two profiles are of different devices: /device:TPU:24 before, /device:TPU:1 now
where the time goes in v1:
time: 692 us
  waiting for transfers between devices  384 us (55%)
  blocking collectives  245 us (35%)
  starting transfers between devices  31.5 us (5%)
  matrix products  9.88 us (1%)
  other arithmetic  9.6 us (1%)
  local copies, waits for them, and re-layouts  9.47 us (1%)
    ppermute x4, waiting for transfers between devices, from_behind(): return lax.ppermute(block, axis, route)  384 us
    unnamed x2, blocking collectives  180 us
    pmax x4, blocking collectives, by_axis(): shard = lax.pmax(shard, axis)  50.6 us
    all_to_all x1, starting transfers between devices, exchange_gather(): blocks = lax.all_to_all(blocks, mesh_axis, split_axis=0, concat_axis=0)  19.4 us
    all_to_all x2, blocking collectives, from_everyone(): return lax.all_to_all(copies, axis, split_axis=0, concat_axis=0, tiled=True)  14.1 us
  transfers between devices with their start and end apart: 5, of which 3 were waited for; matrix products, arithmetic and copies ran while one was open for 1% of the time, Pallas kernels for 0%

profile of v1, /device:TPU:1, one launch (start us, length us, event | category | flops | bytes accessed | tf_op | source)
XLA Modules:
  0.0 691.7 jit_solution(9764749307576593477)
XLA Ops:
  1.6 1.3 select_reduce_fusion.6
  2.9 4.6 collective-permute-start
  7.5 0.8 copy.14
  8.5 1.9 collective-permute-start.2
  10.6 1.3 collective-permute-done
  12.5 0.8 select_reduce_fusion.5
  14.9 7.1 %all_to_all.16 = bf16[4,16,896]{2,1,0:T(8,128)(2,1)S(1)} all-to-all(bf16[4,16,896]{2,1,0:T(8,128)(2,1)S(1)} %broadcast_in_dim.150), channel_id=1, replica_groups=mesh['dp_0'=8,'dp_1'=8,'dp_2'=2,'tensor'=4] {'tensor'}, dimensions={0} | all-to-all | bytes 229376 | tf_op jit(solution)/shard_map/all_to_all | solution.py:28
  22.2 0.8 multiply_convert_fusion
  23.0 7.0 %stack.2 = bf16[128,16,3584]{2,1,0:T(8,128)(2,1)} broadcast(bf16[16,3584]{1,0:T(8,128)(2,1)S(1)} %multiply_convert_fusion), dimensions={1,2} | broadcast | bytes 14794752 | tf_op jit(solution)/shard_map/stack | solution.py:15
  30.0 19.4 %all-to-all-start.1 = ((bf16[128,16,3584]{2,1,0:T(8,128)(2,1)}), bf16[128,16,3584]{2,1,0:T(8,128)(2,1)}, u32[]{:S(2)}, u32[]{:S(2)}) async-start(bf16[128,16,3584]{2,1,0:T(8,128)(2,1)} %stack.2), calls=%async_computation.1 | async-start | bytes 29360128 | tf_op jit(solution)/shard_map/all_to_all | solution.py:16
  49.6 3.5 collective-permute-start.3
  53.1 2.0 collective-permute-start.1
  55.2 1.3 dynamic-slice
  57.4 381.8 %collective-permute-done.1 = s32[1]{0:T(128)} collective-permute-done((s32[1]{0:T(128)}, s32[1]{0:T(128)}, u32[]{:S(2)}, u32[]{:S(2)}) %collective-permute-start.1) | collective-permute-done | bytes 36 | tf_op jit(solution)/shard_map/ppermute | solution.py:23
  440.2 83.6 %all-reduce = s32[2048]{0:T(1024)S(1)} all-reduce(s32[2048]{0:T(1024)S(1)} %add_dynamic-update-slice_fusion), channel_id=1, replica_groups=mesh['dp_0'=8,'dp_1'=8,'dp_2'=2,'tensor'=4] {'dp_0','dp_1','dp_2'}, use_global_device_ids=true, to_apply=%add | all-reduce | flops 2048 | bytes 16384
  523.8 9.6 %fusion.9 = (f32[2048]{0:T(1024)S(1)}, f32[2048,297]{0,1:T(8,128)}) fusion(bf16[2048,3584]{1,0:T(8,128)(2,1)} %bitcast.11, bf16[297,3584]{1,0:T(8,128)(2,1)S(1)} %copy-done), kind=kOutput, calls=%fused_computation.51 | convolution fusion | flops 4360585216 | bytes 19250176 | tf_op jit(solution)/shard_map/dot_general | solution.py:62
  533.4 12.3 %pmax.28 = f32[2048]{0:T(1024)S(1)} all-reduce(f32[2048]{0:T(1024)S(1)} %get-tuple-element.20), channel_id=1, replica_groups=mesh['dp_0'=8,'dp_1'=8,'dp_2'=2,'tensor'=4] {'dp_0'}, use_global_device_ids=true, to_apply=%region_9.10 | all-reduce | flops 2048 | bytes 16384 | tf_op jit(solution)/shard_map/pmax | solution.py:44
  545.8 16.7 %pmax.29 = f32[2048]{0:T(1024)S(1)} all-reduce(f32[2048]{0:T(1024)S(1)} %pmax.28), channel_id=1, replica_groups=mesh['dp_0'=8,'dp_1'=8,'dp_2'=2,'tensor'=4] {'dp_1'}, use_global_device_ids=true, to_apply=%region_10.11 | all-reduce | flops 2048 | bytes 16384 | tf_op jit(solution)/shard_map/pmax | solution.py:44
  562.5 14.6 %pmax.30 = f32[2048]{0:T(1024)S(1)} all-reduce(f32[2048]{0:T(1024)S(1)} %pmax.29), channel_id=1, replica_groups=mesh['dp_0'=8,'dp_1'=8,'dp_2'=2,'tensor'=4] {'dp_2'}, use_global_device_ids=true, to_apply=%region_11.12 | all-reduce | flops 2048 | bytes 16384 | tf_op jit(solution)/shard_map/pmax | solution.py:44
  577.1 7.0 %pmax.31 = f32[2048]{0:T(1024)S(1)} all-reduce(f32[2048]{0:T(1024)S(1)} %pmax.30), channel_id=1, replica_groups=mesh['dp_0'=8,'dp_1'=8,'dp_2'=2,'tensor'=4] {'tensor'}, use_global_device_ids=true, to_apply=%region_12.13 | all-reduce | flops 2048 | bytes 16384 | tf_op jit(solution)/shard_map/pmax | solution.py:44
  584.1 2.5 fusion
  586.6 96.8 %all-reduce.4 = (f32[2048]{0:T(1024)S(1)}, f32[2048]{0:T(1024)S(1)}, f32[2048]{0:T(1024)S(1)}) all-reduce(f32[2048]{0:T(1024)S(1)} %get-tuple-element.7, f32[2048]{0:T(1024)S(1)} %get-tuple-element.17, f32[2048]{0:T(1024)S(1)} %get-tuple-element.16), channel_id=4, replica_groups=mesh['dp_0'=8,'dp_1'=8,'dp_2'=2,'tensor'=4] {'dp_0','dp_1','dp_2','tensor'}, use_global_device_ids=true, to_apply=%region_19.20.clone | all-reduce | flops 6144 | bytes 49152
  683.6 7.0 %all_to_all.17 = f32[4,1,2]{2,1,0:T(1,128)S(1)} all-to-all(f32[4,1,2]{2,1,0:T(1,128)S(1)} %broadcast_in_dim.163), channel_id=1, replica_groups=mesh['dp_0'=8,'dp_1'=8,'dp_2'=2,'tensor'=4] {'tensor'}, dimensions={0} | all-to-all | bytes 64 | tf_op jit(solution)/shard_map/all_to_all | solution.py:28
  690.6 1.1 convert_divide_fusion
  (40 shorter events, 4.3 us)
Async XLA Ops:
  0.0 523.8 %copy-start = (bf16[297,3584]{1,0:T(8,128)(2,1)S(1)}, bf16[297,3584]{1,0:T(8,128)(2,1)}, u32[]{:S(2)}) copy-start(bf16[297,3584]{1,0:T(8,128)(2,1)} %param.9) | copy-start | bytes 6386692
  2.9 8.9 %collective-permute-start = (s32[1]{0:T(128)}, s32[1]{0:T(128)}, u32[]{:S(2)}, u32[]{:S(2)}) collective-permute-start(s32[1]{0:T(128)} %bitcast.1), channel_id=1, source_target_pairs={{0,4},{4,8},{8,12},{12,16},{16,20},{20,24},{24,28},{28,32},{32,36}... | collective-permute-start | bytes 20 | tf_op jit(solution)/shard_map/ppermute | solution.py:23
  8.5 6.1 collective-permute-start.2
  30.0 19.5 %copy-start.1 = (s32[4,8]{1,0:T(4,128)S(1)}, s32[4,8]{1,0:T(4,128)}, u32[]{:S(2)}) copy-start(s32[4,8]{1,0:T(4,128)} %param.13) | copy-start | bytes 388
  30.0 493.8 %all-to-all-start.1 = ((bf16[128,16,3584]{2,1,0:T(8,128)(2,1)}), bf16[128,16,3584]{2,1,0:T(8,128)(2,1)}, u32[]{:S(2)}, u32[]{:S(2)}) async-start(bf16[128,16,3584]{2,1,0:T(8,128)(2,1)} %stack.2), calls=%async_computation.1 | async-start | bytes 29360128 | tf_op jit(solution)/shard_map/all_to_all | solution.py:16
  49.6 390.4 %collective-permute-start.3 = (s32[1,8]{1,0:T(1,128)S(1)}, s32[1,8]{1,0:T(1,128)S(1)}, u32[]{:S(2)}, u32[]{:S(2)}) collective-permute-start(s32[1,8]{1,0:T(1,128)S(1)} %bitcast.37), channel_id=1, source_target_pairs={{0,4},{4,8},{8,12},{12,16},{16,20},{20,24},{24,28},{28,32},{32,36}... | collective-permute-start | bytes 104 | tf_op jit(solution)/shard_map/ppermute | solution.py:23
  53.1 386.1 %collective-permute-start.1 = (s32[1]{0:T(128)}, s32[1]{0:T(128)}, u32[]{:S(2)}, u32[]{:S(2)}) collective-permute-start(s32[1]{0:T(128)} %bitcast.3), channel_id=1, source_target_pairs={{0,4},{4,8},{8,12},{12,16},{16,20},{20,24},{24,28},{28,32},{32,36}... | collective-permute-start | bytes 20 | tf_op jit(solution)/shard_map/ppermute | solution.py:23
